TPU v7x, 32 devices: a whole 2x2x4 slice. The times are simulated.
32 devices in a mesh: dp: 8 (over z, y), blk: 4 (over x, core).
Axes of the slice: x: 2, y: 2, z: 4, core: 2. Of those that a mesh axis runs over, the one named last changes fastest.
Arguments:
- tokens: bfloat16 [4096, 4096], P(('dp', 'blk')), may hold values from -6 to 6
- gate_projection_weight: bfloat16 [4096, 7168], P(None, 'blk'), may hold values from -0.09375 to 0.09375
- up_projection_weight: bfloat16 [4096, 7168], P('dp', 'blk'), may hold values from -0.09375 to 0.09375
- down_projection_weight: bfloat16 [7168, 4096], P('blk', 'dp'), may hold values from -0.0625 to 0.0625
- router_projection_weight: bfloat16 [4096, 8], replicated, may hold values from -0.09375 to 0.09375
- adapter_down_factors: bfloat16 [4096, 128], replicated, may hold values from -0.09375 to 0.09375
- adapter_up_factors: bfloat16 [128, 4096], replicated, may hold values from -1.5 to 1.5
- routes: int32 [4096, 2], P(('dp', 'blk')), may hold values from 0 to 7, all different within a row
- padding_token_mask: int32 [4096], P(('dp', 'blk')), may hold values 0 or 1
- cotangent: bfloat16 [4096, 4096], P(('dp', 'blk')), may hold values from -6 to 6
Outputs:
- layer_out: bfloat16 [4096, 4096], P(('dp', 'blk'))
- grad_down: float32 [4096, 128], replicated
- grad_up: float32 [128, 4096], replicated
Inputs may be any that keep to these rules, and one draw needn't show every extreme that they name: `routes`: the two experts of a token differ.
All inputs are finite; a program needn't handle non-finite values. No bound on the sum of `padding_token_mask` on one device may be relied on, other than what follows from the above.
Results may differ from a plain program's by a relative error of at most 0.0075.
Values may be sent and summed in bfloat16 or wider, within the bound.
A program may use at most 192 MiB of HBM per device.

v0:
```python
import jax
import jax.numpy as jnp
from jax import lax
from jax.sharding import PartitionSpec as P


def shards(
    tokens,
    gate_projection_weight,
    up_projection_weight,
    down_projection_weight,
    router_projection_weight,
    adapter_down_factors,
    adapter_up_factors,
    routes,
    padding_token_mask,
    cotangent,
):
    grouped = lax.all_gather(tokens, "blk", axis=0, tiled=True)
    gate_act = jnp.dot(grouped, gate_projection_weight, preferred_element_type=jnp.float32)
    up_act = jnp.dot(
        grouped,
        lax.all_gather(up_projection_weight, "dp", axis=0, tiled=True),
        preferred_element_type=jnp.float32,
    )
    down_full = lax.all_gather(down_projection_weight, "dp", axis=1, tiled=True)
    hidden = (jax.nn.silu(gate_act) * up_act).astype(jnp.bfloat16)
    part = jnp.dot(hidden, down_full, preferred_element_type=jnp.float32)
    part = lax.optimization_barrier(part.astype(jnp.bfloat16))
    base = lax.psum_scatter(
        part.astype(jnp.float32).astype(jnp.bfloat16), "blk", scatter_dimension=0, tiled=True
    ).astype(jnp.float32)
    expert_list = router_projection_weight.shape[1]
    rank_index = adapter_down_factors.shape[1] // expert_list
    logits = jnp.dot(tokens, router_projection_weight, preferred_element_type=jnp.float32)
    experts_iota = jnp.arange(expert_list, dtype=jnp.int32)[None, :]
    first_hot = (routes[:, 0:1] == experts_iota).astype(jnp.float32)
    second_hot = (routes[:, 1:2] == experts_iota).astype(jnp.float32)
    first_logit = jnp.sum(logits * first_hot, axis=1, keepdims=True)
    second_logit = jnp.sum(logits * second_hot, axis=1, keepdims=True)
    weight_first = jax.nn.sigmoid(first_logit - second_logit)
    coeff = weight_first * first_hot + (1.0 - weight_first) * second_hot
    coeff_wide = jnp.repeat(coeff, rank_index, axis=1)
    low_rank_state = jnp.dot(tokens, adapter_down_factors, preferred_element_type=jnp.float32)
    scaled_output = (low_rank_state * coeff_wide).astype(jnp.bfloat16)
    adapter_delta = jnp.dot(scaled_output, adapter_up_factors, preferred_element_type=jnp.float32)
    layer_out = (base + adapter_delta).astype(jnp.bfloat16)
    masked_tokens = cotangent * padding_token_mask[:, None].astype(jnp.bfloat16)
    low_rank_gradient = lax.dot_general(
        masked_tokens,
        adapter_up_factors,
        (((1,), (1,)), ((), ())),
        preferred_element_type=jnp.float32,
    )
    dlow = (low_rank_gradient * coeff_wide).astype(jnp.bfloat16)
    local_live = jnp.sum(padding_token_mask.astype(jnp.float32))
    local_up = lax.dot_general(
        scaled_output, masked_tokens, (((0,), (0,)), ((), ())), preferred_element_type=jnp.float32
    )
    local_down = lax.dot_general(
        tokens, dlow, (((0,), (0,)), ((), ())), preferred_element_type=jnp.float32
    )
    summed_down, summed_up, live_total = lax.psum((local_down, local_up, local_live), ("dp", "blk"))
    inverse = 1.0 / jnp.maximum(live_total, 1.0)
    grad_down = summed_down * inverse
    grad_up = summed_up * inverse
    return (layer_out, grad_down, grad_up)


def solution(mesh):
    return jax.shard_map(
        shards,
        mesh=mesh,
        in_specs=(
            P(("dp", "blk"), None),
            P(None, "blk"),
            P("dp", "blk"),
            P("blk", "dp"),
            P(),
            P(),
            P(),
            P(("dp", "blk"), None),
            P(("dp", "blk")),
            P(("dp", "blk"), None),
        ),
        out_specs=(P(("dp", "blk"), None), P(), P()),
        check_vma=False,
    )
```

profile of v0, /device:TPU:0, one launch (start us, length us, event | category | flops | bytes accessed | tf_op | source)
XLA Modules:
  0.0 549.2 jit_solution(12669758104570332105)
XLA Ops:
  8.0 0.0 copy-start
  8.0 0.0 copy-start.1
  8.0 0.0 copy-start.4
  8.0 0.0 copy-start.3
  8.0 0.0 copy-start.5
  8.1 0.0 all-gather.4.cloned.1.call-start
  8.1 0.7 all-gather.4.cloned.1.call-update
  8.8 0.0 copy-start.2
  8.8 0.0 all-gather.8.cloned.1.call-start
  8.8 0.7 all-gather.8.cloned.1.call-update
  9.5 0.0 all-gather.6.cloned.1.call-start
  9.6 0.7 all-gather.6.cloned.1.call-update
  10.3 0.0 all-reduce.3.cloned.1.call-start
  10.3 0.0 copy-done.4
  10.4 0.0 copy-done.1
  10.4 0.0 copy-done.3
  10.4 0.4 select_reduce_fusion
  10.8 0.1 copy.15
  10.9 0.0 copy-done.5
  10.9 1.6 fusion.2
  12.6 0.0 copy-done.2
  12.6 1.8 fusion.4
  14.4 0.0 copy-done
  14.4 2.7 convolution_bitcast_fusion
  17.1 0.0 all-reduce.3.cloned.1.call-update
  17.2 0.2 reduce-scatter.2.cloned.1.call-start
  17.4 30.6 %all-gather.4.cloned.1.call-done = bf16[512,4096]{1,0:T(8,128)(2,1)} async-done(((bf16[128,4096]{1,0:T(8,128)(2,1)}), bf16[512,4096]{1,0:T(8,128)(2,1)}) %all-gather.4.cloned.1.call-update) | async-done | bytes 4194320 | tf_op jit(solution)/shard_map/all_gather | solution.py:19
  48.0 14.8 %fusion.12 = f32[512,1792]{1,0:T(8,128)} fusion(bf16[512,4096]{1,0:T(8,128)(2,1)} %all-gather.4.cloned.1.call-done, bf16[4096,1792]{1,0:T(8,128)(2,1)} %param.11), kind=kOutput, calls=%fused_computation.28 | convolution fusion | flops 7516192768 | bytes 22544384 | tf_op jit(solution)/shard_map/dot_general | solution.py:20
  62.7 195.0 %all-gather.8.cloned.1.call-done = bf16[1792,4096]{1,0:T(8,128)(2,1)} async-done(((bf16[1792,512]{1,0:T(8,128)(2,1)}), bf16[1792,4096]{1,0:T(8,128)(2,1)}) %all-gather.8.cloned.1.call-update) | async-done | bytes 14680080 | tf_op jit(solution)/shard_map/all_gather | solution.py:26
  257.7 204.7 %all-gather.6.cloned.1.call-done = bf16[4096,1792]{1,0:T(8,128)(2,1)} async-done(((bf16[512,1792]{1,0:T(8,128)(2,1)}), bf16[4096,1792]{1,0:T(8,128)(2,1)}) %all-gather.6.cloned.1.call-update) | async-done | bytes 14680080 | tf_op jit(solution)/shard_map/all_gather | solution.py:23
  462.4 29.0 %convolution_convert_fusion = bf16[512,4096]{1,0:T(8,128)(2,1)} fusion(bf16[1792,4096]{1,0:T(8,128)(2,1)} %all-gather.8.cloned.1.call-done, f32[512,1792]{1,0:T(8,128)} %fusion.12, bf16[512,4096]{1,0:T(8,128)(2,1)} %all-gather.4.cloned.1.call-done, bf16[4096,1792]{1,0:T(8,128)(2,1)} %all-gather.6.cloned.1.call-done), kind=kOutput, calls=%fused_computation | convolution fusion | flops 15039987712 | bytes 41418752 | tf_op jit(solution)/shard_map/dot_general | solution.py:28
  491.3 0.0 reduce-scatter.2.cloned.1.call-update
  491.4 0.6 convert_reduce_fusion
  492.0 40.0 %psum.22 = f32[]{:T(128)} all-reduce(f32[]{:T(128)} %convert_reduce_fusion), channel_id=1, replica_groups=mesh['dp'=8,'blk'=4] {'dp','blk'}, use_global_device_ids=true, to_apply=%region_5.6 | all-reduce | flops 1 | bytes 8 | tf_op jit(solution)/shard_map/psum | solution.py:63
  532.7 0.0 all-reduce.3.cloned.1.call-done
  532.7 1.8 broadcast_multiply_fusion.1
  534.5 1.8 copy.16
  536.3 3.1 broadcast_multiply_fusion
  539.4 0.0 reduce-scatter.2.cloned.1.call-done
  539.4 2.6 fusion
  (5 shorter events, 0.0 us)
Async XLA Ops:
  8.0 6.4 %copy-start = (bf16[128,4096]{1,0:T(8,128)(2,1)S(1)}, bf16[128,4096]{1,0:T(8,128)(2,1)}, u32[]{:S(2)}) copy-start(bf16[128,4096]{1,0:T(8,128)(2,1)} %param.16) | copy-start | bytes 3145732
  8.0 2.3 copy-start.1
  8.0 2.3 copy-start.4
  8.0 2.3 copy-start.3
  8.0 2.9 copy-start.5
  8.1 39.9 %all-gather.4.cloned.1.call-start = ((), (), s32[]{:S(2)}) async-start(), calls=%async_computation.1 | async-start | bytes 5242880 | tf_op jit(solution)/shard_map/all_gather | solution.py:19
  8.8 3.8 copy-start.2
  8.8 248.9 %all-gather.8.cloned.1.call-start = ((), (), s32[]{:S(2)}) async-start(), calls=%async_computation.3 | async-start | bytes 16515072 | tf_op jit(solution)/shard_map/all_gather | solution.py:26
  9.5 452.8 %all-gather.6.cloned.1.call-start = ((), (), s32[]{:S(2)}) async-start(), calls=%async_computation.2 | async-start | bytes 16515072 | tf_op jit(solution)/shard_map/all_gather | solution.py:23
  10.3 522.5 %all-reduce.3.cloned.1.call-start = ((), (), s32[]{:S(2)}) async-start(), calls=%async_computation.5 | async-start | bytes 8388608 | tf_op jit(solution)/shard_map/psum | solution.py:63
  17.2 522.3 %reduce-scatter.2.cloned.1.call-start = ((), (), s32[]{:S(2)}) async-start(), calls=%async_computation.4 | async-start | bytes 5242880 | tf_op jit(solution)/shard_map/reduce_scatter | solution.py:30
Sparse Core Ops, SparseCore 0:
  10.4 37.5 all-gather.3
  50.0 207.6 all-gather.7
  259.9 202.4 all-gather.5
  491.5 44.3 reduce-scatter.1
Sparse Core Ops, SparseCore 1:
  17.2 482.6 all-reduce.2
where the time goes:
time: 550 us; the launch traced here: 549 us
  waiting for transfers between devices  432 us (79%)
  matrix products  52.9 us (10%)
  blocking collectives  40 us (7%)
  between operations  16.1 us (3%)
    all_gather x1, waiting for transfers between devices, shards(): lax.all_gather(up_projection_weight, 'dp', axis=0, tiled=True)  205 us
    all_gather x1, waiting for transfers between devices, shards(): down_full = lax.all_gather(down_projection_weight, 'dp', axis=1, tiled=True)  195 us
    psum x1, blocking collectives, shards(): lax.psum((local_down, local_up, local_live), ('dp', 'blk'))  40 us
    all_gather x1, waiting for transfers between devices, shards(): grouped = lax.all_gather(tokens, 'blk', axis=0, tiled=True)  30.6 us
    dot_general x1, matrix products, shards(): part = jnp.dot(hidden, down_full, preferred_element_type=jnp.float32)  29 us
    dot_general x1, matrix products, shards(): jnp.dot(grouped, gate_projection_weight, preferred_element_type=jnp.float32)  14.8 us
  transfers between devices with their start and end apart: 5, of which 3 were waited for; matrix products, arithmetic and copies ran while one was open for 11% of the time, Pallas kernels for 0%

commit v1 on v0

--- a/solution.py
+++ b/solution.py
@@ -60,7 +60,9 @@
     local_down = lax.dot_general(
         tokens, dlow, (((0,), (0,)), ((), ())), preferred_element_type=jnp.float32
     )
-    summed_down, summed_up, live_total = lax.psum((local_down, local_up, local_live), ("dp", "blk"))
+    summed_down, summed_up, live_total = lax.psum(
+        lax.psum((local_down, local_up, local_live), "blk"), "dp"
+    )
     inverse = 1.0 / jnp.maximum(live_total, 1.0)
     grad_down = summed_down * inverse
     grad_up = summed_up * inverse

time: 550 us -> 762 us (1.39)
  waiting for transfers between devices: 432 us -> 655 us
  blocking collectives: 40 us -> 27 us
    psum x1 -> x2, waiting for transfers between devices: 0.03 us -> 186 us  [the longest x1 100 us: shards(): lax.psum(lax.psum((local_down, local_up, local_live), 'blk'), 'dp')]
    reduce_scatter x1, waiting for transfers between devices: 0.01 us -> 39.3 us  [shards(): lax.psum_scatter(part.astype(jnp.float32).astype(jnp.bfloat16), 'blk', sc...]
    psum x1 -> x2, blocking collectives: 40 us -> 27 us  [the longest x1 20.1 us: shards(): lax.psum(lax.psum((local_down, local_up, local_live), 'blk'), 'dp')]
  transfers between devices with their start and end apart: 5 -> 6, of which waited for: 3 -> 6; matrix products, arithmetic and copies ran while one was open for 11% -> 7% of each run, Pallas kernels for 0% -> 0%
where the time goes in v1:
time: 762 us; the launch traced here: 761 us
  waiting for transfers between devices  655 us (86%)
  matrix products  54.8 us (7%)
  blocking collectives  27 us (4%)
  between operations  14.9 us (2%)
    all_gather x1, waiting for transfers between devices, shards(): lax.all_gather(up_projection_weight, 'dp', axis=0, tiled=True)  202 us
    all_gather x1, waiting for transfers between devices, shards(): down_full = lax.all_gather(down_projection_weight, 'dp', axis=1, tiled=True)  189 us
    psum x1, waiting for transfers between devices, shards(): lax.psum(lax.psum((local_down, local_up, local_live), 'blk'), 'dp')  100 us
    psum x1, waiting for transfers between devices, shards(): lax.psum((local_down, local_up, local_live), 'blk')  86.3 us
    reduce_scatter x1, waiting for transfers between devices, shards(): lax.psum_scatter(part.astype(jnp.float32).astype(jnp.bfloat16), 'blk', sc...  39.3 us
    all_gather x1, waiting for transfers between devices, shards(): grouped = lax.all_gather(tokens, 'blk', axis=0, tiled=True)  35.9 us
    dot_general x1, matrix products, shards(): part = jnp.dot(hidden, down_full, preferred_element_type=jnp.float32)  29.6 us
    psum x1, blocking collectives, shards(): lax.psum(lax.psum((local_down, local_up, local_live), 'blk'), 'dp')  20.1 us
  transfers between devices with their start and end apart: 6, of which 6 were waited for; matrix products, arithmetic and copies ran while one was open for 7% of the time, Pallas kernels for 0%

profile of v1, /device:TPU:0, one launch (start us, length us, event | category | flops | bytes accessed | tf_op | source)
XLA Modules:
  0.0 761.4 jit_solution(6306874284016280683)
XLA Ops:
  7.2 0.0 copy-start
  7.2 0.0 copy-start.1
  7.2 0.0 copy-start.2
  7.2 0.0 all-reduce.7.cloned.1.call-start
  7.2 0.9 slice_bitcast_fusion.1
  8.1 1.7 select_reduce_fusion
  9.8 0.1 copy.15
  9.9 0.7 convert_element_type.34
  10.6 2.0 fusion.2
  12.5 0.0 copy-done
  12.6 0.0 copy-done.1
  12.6 0.0 copy-done.2
  12.6 2.7 convolution_bitcast_fusion
  15.3 1.8 fusion.4
  17.1 0.0 all-reduce.7.cloned.1.call-update
  17.1 0.0 all-gather.4.cloned.1.call-start
  17.2 0.7 all-gather.4.cloned.1.call-update
  17.9 0.0 all-gather.8.cloned.1.call-start
  17.9 0.7 all-gather.8.cloned.1.call-update
  18.6 0.0 all-gather.6.cloned.1.call-start
  18.7 0.5 all-gather.6.cloned.1.call-update
  19.2 0.0 all-reduce.5.cloned.1.call-start
  19.2 86.3 %all-reduce.7.cloned.1.call-done = (f32[4096,128]{0,1:T(8,128)}, f32[128,4096]{1,0:T(8,128)}) async-done(((f32[4096,128]{0,1:T(8,128)}, f32[128,4096]{1,0:T(8,128)}), (f32[4096,128]{0,1:T(8,128)}, f32[128,4096]{1,0:T(8,128)})) %all-reduce.7.cloned.1.call-update) | async-done | bytes 4194320 | tf_op jit(solution)/shard_map/psum | solution.py:64
  105.5 0.0 all-reduce.5.cloned.1.call-update
  105.5 0.2 reduce-scatter.2.cloned.1.call-start
  105.8 35.9 %all-gather.4.cloned.1.call-done = bf16[512,4096]{1,0:T(8,128)(2,1)} async-done(((bf16[128,4096]{1,0:T(8,128)(2,1)}), bf16[512,4096]{1,0:T(8,128)(2,1)}) %all-gather.4.cloned.1.call-update) | async-done | bytes 4194320 | tf_op jit(solution)/shard_map/all_gather | solution.py:19
  141.7 14.5 %fusion.12 = f32[512,1792]{1,0:T(8,128)} fusion(bf16[512,4096]{1,0:T(8,128)(2,1)} %all-gather.4.cloned.1.call-done, bf16[4096,1792]{1,0:T(8,128)(2,1)} %param.11), kind=kOutput, calls=%fused_computation.28 | convolution fusion | flops 7516192768 | bytes 22544384 | tf_op jit(solution)/shard_map/dot_general | solution.py:20
  156.2 189.3 %all-gather.8.cloned.1.call-done = bf16[1792,4096]{1,0:T(8,128)(2,1)} async-done(((bf16[1792,512]{1,0:T(8,128)(2,1)}), bf16[1792,4096]{1,0:T(8,128)(2,1)}) %all-gather.8.cloned.1.call-update) | async-done | bytes 14680080 | tf_op jit(solution)/shard_map/all_gather | solution.py:26
  345.5 201.9 %all-gather.6.cloned.1.call-done = bf16[4096,1792]{1,0:T(8,128)(2,1)} async-done(((bf16[512,1792]{1,0:T(8,128)(2,1)}), bf16[4096,1792]{1,0:T(8,128)(2,1)}) %all-gather.6.cloned.1.call-update) | async-done | bytes 14680080 | tf_op jit(solution)/shard_map/all_gather | solution.py:23
  547.4 29.6 %convolution_convert_fusion = bf16[512,4096]{1,0:T(8,128)(2,1)} fusion(bf16[1792,4096]{1,0:T(8,128)(2,1)} %all-gather.8.cloned.1.call-done, f32[512,1792]{1,0:T(8,128)} %fusion.12, bf16[512,4096]{1,0:T(8,128)(2,1)} %all-gather.4.cloned.1.call-done, bf16[4096,1792]{1,0:T(8,128)(2,1)} %all-gather.6.cloned.1.call-done), kind=kOutput, calls=%fused_computation | convolution fusion | flops 15039987712 | bytes 41418752 | tf_op jit(solution)/shard_map/dot_general | solution.py:28
  577.0 0.0 copy-start.3
  577.0 0.0 reduce-scatter.2.cloned.1.call-update
  577.0 0.6 copy-done.3
  577.7 0.6 convert_reduce_fusion
  578.3 6.8 psum.44
  585.1 20.1 %psum.45 = f32[]{:T(128)} all-reduce(f32[]{:T(128)} %psum.44), channel_id=1, replica_groups=mesh['dp'=8,'blk'=4] {'dp'}, use_global_device_ids=true, to_apply=%region_7.8 | all-reduce | flops 1 | bytes 8 | tf_op jit(solution)/shard_map/psum | solution.py:63
  605.9 100.0 %all-reduce.5.cloned.1.call-done = (f32[4096,128]{0,1:T(8,128)}, f32[128,4096]{1,0:T(8,128)}) async-done(((f32[4096,128]{0,1:T(8,128)}, f32[128,4096]{1,0:T(8,128)}), (f32[4096,128]{0,1:T(8,128)}, f32[128,4096]{1,0:T(8,128)})) %all-reduce.5.cloned.1.call-update) | async-done | bytes 4194320 | tf_op jit(solution)/shard_map/psum | solution.py:63
  705.9 1.8 broadcast_multiply_fusion.1
  707.7 1.8 copy.16
  709.5 3.1 broadcast_multiply_fusion
  712.6 39.3 %reduce-scatter.2.cloned.1.call-done = bf16[128,4096]{1,0:T(8,128)(2,1)} async-done(((bf16[512,4096]{1,0:T(8,128)(2,1)}), bf16[128,4096]{1,0:T(8,128)(2,1)}) %reduce-scatter.2.cloned.1.call-update) | async-done | bytes 1048592 | tf_op jit(solution)/shard_map/reduce_scatter | solution.py:30
  751.9 2.6 fusion
  (3 shorter events, 0.0 us)
Async XLA Ops:
  7.2 5.4 copy-start
  7.2 5.4 copy-start.1
  7.2 5.4 copy-start.2
  7.2 98.3 %all-reduce.7.cloned.1.call-start = ((), (), s32[]{:S(2)}) async-start(), calls=%async_computation.6 | async-start | bytes 8388608 | tf_op jit(solution)/shard_map/psum | solution.py:64
  17.1 124.6 %all-gather.4.cloned.1.call-start = ((), (), s32[]{:S(2)}) async-start(), calls=%async_computation.1 | async-start | bytes 5242880 | tf_op jit(solution)/shard_map/all_gather | solution.py:19
  17.9 327.6 %all-gather.8.cloned.1.call-start = ((), (), s32[]{:S(2)}) async-start(), calls=%async_computation.3 | async-start | bytes 16515072 | tf_op jit(solution)/shard_map/all_gather | solution.py:26
  18.6 528.8 %all-gather.6.cloned.1.call-start = ((), (), s32[]{:S(2)}) async-start(), calls=%async_computation.2 | async-start | bytes 16515072 | tf_op jit(solution)/shard_map/all_gather | solution.py:23
  19.2 686.7 %all-reduce.5.cloned.1.call-start = ((), (), s32[]{:S(2)}) async-start(), calls=%async_computation.5 | async-start | bytes 8388608 | tf_op jit(solution)/shard_map/psum | solution.py:63
  105.5 646.4 %reduce-scatter.2.cloned.1.call-start = ((), (), s32[]{:S(2)}) async-start(), calls=%async_computation.4 | async-start | bytes 5242880 | tf_op jit(solution)/shard_map/reduce_scatter | solution.py:30
  577.0 0.7 copy-start.3
Sparse Core Ops, SparseCore 0:
  17.2 88.2 all-reduce.6
  107.1 34.5 all-gather.3
  143.8 201.7 all-gather.7
  347.6 199.8 all-gather.5
  551.0 154.8 all-reduce.4
  708.3 43.5 reduce-scatter.1
